TPU v7x, 32 devices: a whole 2x2x4 slice. The times are simulated.
32 devices in a mesh: prow: 4 (over y, core), pcol: 8 (over z, x).
Axes of the slice: x: 2, y: 2, z: 4, core: 2. Of those that a mesh axis runs over, the one named last changes fastest.
Arguments:
- inverse_cov: bfloat16 [8192, 8192], P('prow', 'pcol'), may hold values from -0.5 to 4.5, as said below
- cosines: float32 [8192, 8192], P('prow', 'pcol'), may hold values from -1 to 1, as said below
- sky_maps: bfloat16 [8192, 192], P('pcol'), may hold values from -6 to 6
Outputs:
- filtered: bfloat16 [8192, 192], P('prow')
- spectra: float32 [64, 192], replicated
Inputs may be any that keep to these rules, and one draw needn't show every extreme that they name: `inverse_cov`: symmetric, with a dominant diagonal. `cosines`: symmetric.
All inputs are finite; a program needn't handle non-finite values.
Results may differ from a plain program's by a relative error of at most 0.0033.
Values may be sent and summed in bfloat16 or wider, within the bound.
A program may use at most 128 MiB of HBM per device.

v0:
```python
import jax
import jax.numpy as jnp
from jax import lax
from jax.sharding import PartitionSpec as P

NPIX = 8192
L = 64
LMIN = 2
GROUP = 4


def next_legendre(previous, current, cosine, degree):
    return ((2.0 * degree - 1.0) * cosine * current - (degree - 1.0) * previous) / degree


def per_device(inverse_cov, cosines, sky_maps):
    cols_here = inverse_cov.shape[1]
    partial_value = jnp.dot(inverse_cov, sky_maps, preferred_element_type=jnp.float32)
    filtered = lax.psum(partial_value, "pcol").astype(jnp.bfloat16)
    column_index = lax.axis_index("pcol")
    full_maps = lax.all_gather(filtered, "prow", axis=0, tiled=True)
    filtered_cols = lax.dynamic_slice_in_dim(full_maps, column_index * cols_here, cols_here, 0)
    rows_f32 = filtered.astype(jnp.float32)
    previous = jnp.ones_like(cosines)
    current = cosines

    def advance(carried, turn_index):
        previous, current = carried
        term_list = []
        weights = []
        for offset in range(GROUP):
            degree = (LMIN + turn_index * GROUP + offset).astype(jnp.float32)
            next_term = next_legendre(previous, current, cosines, degree)
            term_list.append(next_term.astype(jnp.bfloat16))
            weights.append((2.0 * degree + 1.0) / NPIX)
            previous, current = (current, next_term)
        stacked = jnp.stack(term_list)
        product = jnp.einsum(
            "grc,cm->grm", stacked, filtered_cols, preferred_element_type=jnp.float32
        )
        quadratic = jnp.sum(product * rows_f32[None], axis=1)
        return ((previous, current), quadratic * jnp.stack(weights)[:, None])

    carried, partial_spectra = lax.scan(
        advance, (previous, current), jnp.arange(L // GROUP, dtype=jnp.int32)
    )
    spectra = lax.psum(partial_spectra.reshape(L, -1), ("prow", "pcol"))
    return (filtered, spectra)


def solution(mesh):
    in_specs = (P("prow", "pcol"), P("prow", "pcol"), P("pcol", None))
    out_specs = (P("prow", None), P())
    return jax.shard_map(
        per_device, mesh=mesh, in_specs=in_specs, out_specs=out_specs, check_vma=False
    )
```

profile of v0, /device:TPU:0, one launch (start us, length us, event | category | flops | bytes accessed | tf_op | source)
XLA Modules:
  0.0 855.3 jit_solution(4507010402875812031)
XLA Ops:
  11.9 82.8 %all-reduce.1 = bf16[2048,192]{0,1:T(8,128)(2,1)} all-reduce(f32[2048,192]{0,1:T(8,128)S(1)} %fusion.15), channel_id=1, replica_groups=mesh['prow'=4,'pcol'=8] {'pcol'}, use_global_device_ids=true, to_apply=%region_0.0 | all-reduce | flops 393216 | bytes 2359296 | tf_op jit(solution)/shard_map/psum | solution.py:19
  105.7 16.7 %all-gather.2.cloned.1.call-done = bf16[8192,192]{0,1:T(8,128)(2,1)} async-done(((bf16[2048,192]{0,1:T(8,128)(2,1)}), bf16[8192,192]{0,1:T(8,128)(2,1)}) %all-gather.2.cloned.1.call-update) | async-done | bytes 3145744 | tf_op jit(solution)/shard_map/all_gather | solution.py:21
  123.5 684.9 %while.18 = (s32[]{:T(128)}, f32[2048,1024]{1,0:T(8,128)}, f32[2048,1024]{1,0:T(8,128)}, f32[16,4,192]{2,1,0:T(4,128)S(1)}, s32[16]{0:T(128)S(1)}, /*index=5*/f3...) while((s32[]{:T(128)}, f32[2048,1024]{1,0:T(8,128)}, ...), condition=%wide.region_3.4_spmd.clone, body=%wide.region_1.3_spmd.clone.sunk | while | flops 3325034496 | bytes 194916608 | solution.py:44
  162.9 12.4 %convert_bitcast_fusion.6 = (bf16[1,2048,1024]{2,1,0:T(8,128)(2,1)S(1)}, f32[2048,1024]{1,0:T(8,128)S(1)}, bf16[1,2048,1024]{2,1,0:T(8,128)(2,1)}) fusion(f32[]{:T(128)} %bitcast.41, f32[]{:T(128)S(6)} %sub.98, f32[]{:T(128)} %bitcast.42, f32[2048,1024]{1,0:T(8,128)} %get-tuple-element.271, f32[]{:T(128)S(6)} %sub.99, f32[]{:T(128)} %bitcast.43, ...), kind=kLoop, calls=%fused_computation.16.clone.1 | loop fusion | flops 37748736 | bytes 41943076 | tf_op jit(solution)/shard_map/while/body/eval_jaxpr/stack | solution.py:37
  175.3 14.8 %convert_bitcast_fusion.7 = (bf16[1,2048,1024]{2,1,0:T(8,128)(2,1)}, f32[2048,1024]{1,0:T(8,128)}, bf16[1,2048,1024]{2,1,0:T(8,128)(2,1)}) fusion(f32[]{:T(128)} %bitcast.44, f32[]{:T(128)} %bitcast.42, f32[2048,1024]{1,0:T(8,128)} %get-tuple-element.271, f32[]{:T(128)S(6)} %sub.99, f32[]{:T(128)} %bitcast.43, f32[2048,1024]{1,0:T(8,128)} %get-tuple-element.270, ...), kind=kLoop, calls=%fused_computation.15.clone.1 | loop fusion | flops 37748736 | bytes 50331684 | tf_op jit(solution)/shard_map/while/body/eval_jaxpr/stack | solution.py:37
  206.0 12.4 %convert_bitcast_fusion.6 = (bf16[1,2048,1024]{2,1,0:T(8,128)(2,1)S(1)}, f32[2048,1024]{1,0:T(8,128)S(1)}, bf16[1,2048,1024]{2,1,0:T(8,128)(2,1)}) fusion(f32[]{:T(128)} %bitcast.41, f32[]{:T(128)S(6)} %sub.98, f32[]{:T(128)} %bitcast.42, f32[2048,1024]{1,0:T(8,128)} %get-tuple-element.271, f32[]{:T(128)S(6)} %sub.99, f32[]{:T(128)} %bitcast.43, ...), kind=kLoop, calls=%fused_computation.16.clone.1 | loop fusion | flops 37748736 | bytes 41943076 | tf_op jit(solution)/shard_map/while/body/eval_jaxpr/stack | solution.py:37
  218.4 14.8 %convert_bitcast_fusion.7 = (bf16[1,2048,1024]{2,1,0:T(8,128)(2,1)}, f32[2048,1024]{1,0:T(8,128)}, bf16[1,2048,1024]{2,1,0:T(8,128)(2,1)}) fusion(f32[]{:T(128)} %bitcast.44, f32[]{:T(128)} %bitcast.42, f32[2048,1024]{1,0:T(8,128)} %get-tuple-element.271, f32[]{:T(128)S(6)} %sub.99, f32[]{:T(128)} %bitcast.43, f32[2048,1024]{1,0:T(8,128)} %get-tuple-element.270, ...), kind=kLoop, calls=%fused_computation.15.clone.1 | loop fusion | flops 37748736 | bytes 50331684 | tf_op jit(solution)/shard_map/while/body/eval_jaxpr/stack | solution.py:37
  249.1 12.4 %convert_bitcast_fusion.6 = (bf16[1,2048,1024]{2,1,0:T(8,128)(2,1)S(1)}, f32[2048,1024]{1,0:T(8,128)S(1)}, bf16[1,2048,1024]{2,1,0:T(8,128)(2,1)}) fusion(f32[]{:T(128)} %bitcast.41, f32[]{:T(128)S(6)} %sub.98, f32[]{:T(128)} %bitcast.42, f32[2048,1024]{1,0:T(8,128)} %get-tuple-element.271, f32[]{:T(128)S(6)} %sub.99, f32[]{:T(128)} %bitcast.43, ...), kind=kLoop, calls=%fused_computation.16.clone.1 | loop fusion | flops 37748736 | bytes 41943076 | tf_op jit(solution)/shard_map/while/body/eval_jaxpr/stack | solution.py:37
  261.5 14.8 %convert_bitcast_fusion.7 = (bf16[1,2048,1024]{2,1,0:T(8,128)(2,1)}, f32[2048,1024]{1,0:T(8,128)}, bf16[1,2048,1024]{2,1,0:T(8,128)(2,1)}) fusion(f32[]{:T(128)} %bitcast.44, f32[]{:T(128)} %bitcast.42, f32[2048,1024]{1,0:T(8,128)} %get-tuple-element.271, f32[]{:T(128)S(6)} %sub.99, f32[]{:T(128)} %bitcast.43, f32[2048,1024]{1,0:T(8,128)} %get-tuple-element.270, ...), kind=kLoop, calls=%fused_computation.15.clone.1 | loop fusion | flops 37748736 | bytes 50331684 | tf_op jit(solution)/shard_map/while/body/eval_jaxpr/stack | solution.py:37
  292.2 12.4 %convert_bitcast_fusion.6 = (bf16[1,2048,1024]{2,1,0:T(8,128)(2,1)S(1)}, f32[2048,1024]{1,0:T(8,128)S(1)}, bf16[1,2048,1024]{2,1,0:T(8,128)(2,1)}) fusion(f32[]{:T(128)} %bitcast.41, f32[]{:T(128)S(6)} %sub.98, f32[]{:T(128)} %bitcast.42, f32[2048,1024]{1,0:T(8,128)} %get-tuple-element.271, f32[]{:T(128)S(6)} %sub.99, f32[]{:T(128)} %bitcast.43, ...), kind=kLoop, calls=%fused_computation.16.clone.1 | loop fusion | flops 37748736 | bytes 41943076 | tf_op jit(solution)/shard_map/while/body/eval_jaxpr/stack | solution.py:37
  304.6 14.8 %convert_bitcast_fusion.7 = (bf16[1,2048,1024]{2,1,0:T(8,128)(2,1)}, f32[2048,1024]{1,0:T(8,128)}, bf16[1,2048,1024]{2,1,0:T(8,128)(2,1)}) fusion(f32[]{:T(128)} %bitcast.44, f32[]{:T(128)} %bitcast.42, f32[2048,1024]{1,0:T(8,128)} %get-tuple-element.271, f32[]{:T(128)S(6)} %sub.99, f32[]{:T(128)} %bitcast.43, f32[2048,1024]{1,0:T(8,128)} %get-tuple-element.270, ...), kind=kLoop, calls=%fused_computation.15.clone.1 | loop fusion | flops 37748736 | bytes 50331684 | tf_op jit(solution)/shard_map/while/body/eval_jaxpr/stack | solution.py:37
  335.3 12.4 %convert_bitcast_fusion.6 = (bf16[1,2048,1024]{2,1,0:T(8,128)(2,1)S(1)}, f32[2048,1024]{1,0:T(8,128)S(1)}, bf16[1,2048,1024]{2,1,0:T(8,128)(2,1)}) fusion(f32[]{:T(128)} %bitcast.41, f32[]{:T(128)S(6)} %sub.98, f32[]{:T(128)} %bitcast.42, f32[2048,1024]{1,0:T(8,128)} %get-tuple-element.271, f32[]{:T(128)S(6)} %sub.99, f32[]{:T(128)} %bitcast.43, ...), kind=kLoop, calls=%fused_computation.16.clone.1 | loop fusion | flops 37748736 | bytes 41943076 | tf_op jit(solution)/shard_map/while/body/eval_jaxpr/stack | solution.py:37
  347.8 14.8 %convert_bitcast_fusion.7 = (bf16[1,2048,1024]{2,1,0:T(8,128)(2,1)}, f32[2048,1024]{1,0:T(8,128)}, bf16[1,2048,1024]{2,1,0:T(8,128)(2,1)}) fusion(f32[]{:T(128)} %bitcast.44, f32[]{:T(128)} %bitcast.42, f32[2048,1024]{1,0:T(8,128)} %get-tuple-element.271, f32[]{:T(128)S(6)} %sub.99, f32[]{:T(128)} %bitcast.43, f32[2048,1024]{1,0:T(8,128)} %get-tuple-element.270, ...), kind=kLoop, calls=%fused_computation.15.clone.1 | loop fusion | flops 37748736 | bytes 50331684 | tf_op jit(solution)/shard_map/while/body/eval_jaxpr/stack | solution.py:37
  390.9 14.8 %convert_bitcast_fusion.7 = (bf16[1,2048,1024]{2,1,0:T(8,128)(2,1)}, f32[2048,1024]{1,0:T(8,128)}, bf16[1,2048,1024]{2,1,0:T(8,128)(2,1)}) fusion(f32[]{:T(128)} %bitcast.44, f32[]{:T(128)} %bitcast.42, f32[2048,1024]{1,0:T(8,128)} %get-tuple-element.271, f32[]{:T(128)S(6)} %sub.99, f32[]{:T(128)} %bitcast.43, f32[2048,1024]{1,0:T(8,128)} %get-tuple-element.270, ...), kind=kLoop, calls=%fused_computation.15.clone.1 | loop fusion | flops 37748736 | bytes 50331684 | tf_op jit(solution)/shard_map/while/body/eval_jaxpr/stack | solution.py:37
  434.0 14.8 %convert_bitcast_fusion.7 = (bf16[1,2048,1024]{2,1,0:T(8,128)(2,1)}, f32[2048,1024]{1,0:T(8,128)}, bf16[1,2048,1024]{2,1,0:T(8,128)(2,1)}) fusion(f32[]{:T(128)} %bitcast.44, f32[]{:T(128)} %bitcast.42, f32[2048,1024]{1,0:T(8,128)} %get-tuple-element.271, f32[]{:T(128)S(6)} %sub.99, f32[]{:T(128)} %bitcast.43, f32[2048,1024]{1,0:T(8,128)} %get-tuple-element.270, ...), kind=kLoop, calls=%fused_computation.15.clone.1 | loop fusion | flops 37748736 | bytes 50331684 | tf_op jit(solution)/shard_map/while/body/eval_jaxpr/stack | solution.py:37
  477.1 14.8 %convert_bitcast_fusion.7 = (bf16[1,2048,1024]{2,1,0:T(8,128)(2,1)}, f32[2048,1024]{1,0:T(8,128)}, bf16[1,2048,1024]{2,1,0:T(8,128)(2,1)}) fusion(f32[]{:T(128)} %bitcast.44, f32[]{:T(128)} %bitcast.42, f32[2048,1024]{1,0:T(8,128)} %get-tuple-element.271, f32[]{:T(128)S(6)} %sub.99, f32[]{:T(128)} %bitcast.43, f32[2048,1024]{1,0:T(8,128)} %get-tuple-element.270, ...), kind=kLoop, calls=%fused_computation.15.clone.1 | loop fusion | flops 37748736 | bytes 50331684 | tf_op jit(solution)/shard_map/while/body/eval_jaxpr/stack | solution.py:37
  520.2 14.8 %convert_bitcast_fusion.7 = (bf16[1,2048,1024]{2,1,0:T(8,128)(2,1)}, f32[2048,1024]{1,0:T(8,128)}, bf16[1,2048,1024]{2,1,0:T(8,128)(2,1)}) fusion(f32[]{:T(128)} %bitcast.44, f32[]{:T(128)} %bitcast.42, f32[2048,1024]{1,0:T(8,128)} %get-tuple-element.271, f32[]{:T(128)S(6)} %sub.99, f32[]{:T(128)} %bitcast.43, f32[2048,1024]{1,0:T(8,128)} %get-tuple-element.270, ...), kind=kLoop, calls=%fused_computation.15.clone.1 | loop fusion | flops 37748736 | bytes 50331684 | tf_op jit(solution)/shard_map/while/body/eval_jaxpr/stack | solution.py:37
  563.4 14.8 %convert_bitcast_fusion.7 = (bf16[1,2048,1024]{2,1,0:T(8,128)(2,1)}, f32[2048,1024]{1,0:T(8,128)}, bf16[1,2048,1024]{2,1,0:T(8,128)(2,1)}) fusion(f32[]{:T(128)} %bitcast.44, f32[]{:T(128)} %bitcast.42, f32[2048,1024]{1,0:T(8,128)} %get-tuple-element.271, f32[]{:T(128)S(6)} %sub.99, f32[]{:T(128)} %bitcast.43, f32[2048,1024]{1,0:T(8,128)} %get-tuple-element.270, ...), kind=kLoop, calls=%fused_computation.15.clone.1 | loop fusion | flops 37748736 | bytes 50331684 | tf_op jit(solution)/shard_map/while/body/eval_jaxpr/stack | solution.py:37
  606.5 14.8 %convert_bitcast_fusion.7 = (bf16[1,2048,1024]{2,1,0:T(8,128)(2,1)}, f32[2048,1024]{1,0:T(8,128)}, bf16[1,2048,1024]{2,1,0:T(8,128)(2,1)}) fusion(f32[]{:T(128)} %bitcast.44, f32[]{:T(128)} %bitcast.42, f32[2048,1024]{1,0:T(8,128)} %get-tuple-element.271, f32[]{:T(128)S(6)} %sub.99, f32[]{:T(128)} %bitcast.43, f32[2048,1024]{1,0:T(8,128)} %get-tuple-element.270, ...), kind=kLoop, calls=%fused_computation.15.clone.1 | loop fusion | flops 37748736 | bytes 50331684 | tf_op jit(solution)/shard_map/while/body/eval_jaxpr/stack | solution.py:37
  649.6 14.8 %convert_bitcast_fusion.7 = (bf16[1,2048,1024]{2,1,0:T(8,128)(2,1)}, f32[2048,1024]{1,0:T(8,128)}, bf16[1,2048,1024]{2,1,0:T(8,128)(2,1)}) fusion(f32[]{:T(128)} %bitcast.44, f32[]{:T(128)} %bitcast.42, f32[2048,1024]{1,0:T(8,128)} %get-tuple-element.271, f32[]{:T(128)S(6)} %sub.99, f32[]{:T(128)} %bitcast.43, f32[2048,1024]{1,0:T(8,128)} %get-tuple-element.270, ...), kind=kLoop, calls=%fused_computation.15.clone.1 | loop fusion | flops 37748736 | bytes 50331684 | tf_op jit(solution)/shard_map/while/body/eval_jaxpr/stack | solution.py:37
  692.7 14.8 %convert_bitcast_fusion.7 = (bf16[1,2048,1024]{2,1,0:T(8,128)(2,1)}, f32[2048,1024]{1,0:T(8,128)}, bf16[1,2048,1024]{2,1,0:T(8,128)(2,1)}) fusion(f32[]{:T(128)} %bitcast.44, f32[]{:T(128)} %bitcast.42, f32[2048,1024]{1,0:T(8,128)} %get-tuple-element.271, f32[]{:T(128)S(6)} %sub.99, f32[]{:T(128)} %bitcast.43, f32[2048,1024]{1,0:T(8,128)} %get-tuple-element.270, ...), kind=kLoop, calls=%fused_computation.15.clone.1 | loop fusion | flops 37748736 | bytes 50331684 | tf_op jit(solution)/shard_map/while/body/eval_jaxpr/stack | solution.py:37
  735.8 14.8 %convert_bitcast_fusion.7 = (bf16[1,2048,1024]{2,1,0:T(8,128)(2,1)}, f32[2048,1024]{1,0:T(8,128)}, bf16[1,2048,1024]{2,1,0:T(8,128)(2,1)}) fusion(f32[]{:T(128)} %bitcast.44, f32[]{:T(128)} %bitcast.42, f32[2048,1024]{1,0:T(8,128)} %get-tuple-element.271, f32[]{:T(128)S(6)} %sub.99, f32[]{:T(128)} %bitcast.43, f32[2048,1024]{1,0:T(8,128)} %get-tuple-element.270, ...), kind=kLoop, calls=%fused_computation.15.clone.1 | loop fusion | flops 37748736 | bytes 50331684 | tf_op jit(solution)/shard_map/while/body/eval_jaxpr/stack | solution.py:37
  779.0 14.8 %convert_bitcast_fusion.7 = (bf16[1,2048,1024]{2,1,0:T(8,128)(2,1)}, f32[2048,1024]{1,0:T(8,128)}, bf16[1,2048,1024]{2,1,0:T(8,128)(2,1)}) fusion(f32[]{:T(128)} %bitcast.44, f32[]{:T(128)} %bitcast.42, f32[2048,1024]{1,0:T(8,128)} %get-tuple-element.271, f32[]{:T(128)S(6)} %sub.99, f32[]{:T(128)} %bitcast.43, f32[2048,1024]{1,0:T(8,128)} %get-tuple-element.270, ...), kind=kLoop, calls=%fused_computation.15.clone.1 | loop fusion | flops 37748736 | bytes 50331684 | tf_op jit(solution)/shard_map/while/body/eval_jaxpr/stack | solution.py:37
  808.4 40.1 %psum.15 = f32[64,192]{1,0:T(8,128)} all-reduce(f32[64,192]{1,0:T(8,128)S(1)} %reshape.51), channel_id=1, replica_groups=mesh['prow'=4,'pcol'=8] {'prow','pcol'}, use_global_device_ids=true, to_apply=%region_4.5 | all-reduce | flops 12288 | bytes 98304 | tf_op jit(solution)/shard_map/psum | solution.py:47
  (200 shorter events, 406.7 us)
Async XLA Ops:
  7.2 115.2 %all-gather.2.cloned.1.call-start = ((), (), s32[]{:S(2)}) async-start(), calls=%async_computation | async-start | bytes 3932160 | tf_op jit(solution)/shard_map/all_gather | solution.py:21
  124.8 10.9 %copy-start.1 = (f32[2048,1024]{1,0:T(8,128)S(1)}, f32[2048,1024]{1,0:T(8,128)}, u32[]{:S(2)}) copy-start(f32[2048,1024]{1,0:T(8,128)} %get-tuple-element.292) | copy-start | bytes 25165828 | tf_op jit(solution)/shard_map/while
  147.0 6.5 copy-start.3
  162.9 12.4 %copy-start.1 = (f32[2048,1024]{1,0:T(8,128)S(1)}, f32[2048,1024]{1,0:T(8,128)}, u32[]{:S(2)}) copy-start(f32[2048,1024]{1,0:T(8,128)} %get-tuple-element.292) | copy-start | bytes 25165828 | tf_op jit(solution)/shard_map/while
  190.1 6.5 copy-start.3
  206.0 12.4 %copy-start.1 = (f32[2048,1024]{1,0:T(8,128)S(1)}, f32[2048,1024]{1,0:T(8,128)}, u32[]{:S(2)}) copy-start(f32[2048,1024]{1,0:T(8,128)} %get-tuple-element.292) | copy-start | bytes 25165828 | tf_op jit(solution)/shard_map/while
  233.2 6.5 copy-start.3
  249.1 12.4 %copy-start.1 = (f32[2048,1024]{1,0:T(8,128)S(1)}, f32[2048,1024]{1,0:T(8,128)}, u32[]{:S(2)}) copy-start(f32[2048,1024]{1,0:T(8,128)} %get-tuple-element.292) | copy-start | bytes 25165828 | tf_op jit(solution)/shard_map/while
  276.4 6.5 copy-start.3
  292.2 12.4 %copy-start.1 = (f32[2048,1024]{1,0:T(8,128)S(1)}, f32[2048,1024]{1,0:T(8,128)}, u32[]{:S(2)}) copy-start(f32[2048,1024]{1,0:T(8,128)} %get-tuple-element.292) | copy-start | bytes 25165828 | tf_op jit(solution)/shard_map/while
  319.5 6.5 copy-start.3
  335.3 12.4 %copy-start.1 = (f32[2048,1024]{1,0:T(8,128)S(1)}, f32[2048,1024]{1,0:T(8,128)}, u32[]{:S(2)}) copy-start(f32[2048,1024]{1,0:T(8,128)} %get-tuple-element.292) | copy-start | bytes 25165828 | tf_op jit(solution)/shard_map/while
  362.6 6.5 copy-start.3
  378.5 12.4 %copy-start.1 = (f32[2048,1024]{1,0:T(8,128)S(1)}, f32[2048,1024]{1,0:T(8,128)}, u32[]{:S(2)}) copy-start(f32[2048,1024]{1,0:T(8,128)} %get-tuple-element.292) | copy-start | bytes 25165828 | tf_op jit(solution)/shard_map/while
  405.7 6.5 copy-start.3
  421.6 12.4 %copy-start.1 = (f32[2048,1024]{1,0:T(8,128)S(1)}, f32[2048,1024]{1,0:T(8,128)}, u32[]{:S(2)}) copy-start(f32[2048,1024]{1,0:T(8,128)} %get-tuple-element.292) | copy-start | bytes 25165828 | tf_op jit(solution)/shard_map/while
  464.7 12.4 %copy-start.1 = (f32[2048,1024]{1,0:T(8,128)S(1)}, f32[2048,1024]{1,0:T(8,128)}, u32[]{:S(2)}) copy-start(f32[2048,1024]{1,0:T(8,128)} %get-tuple-element.292) | copy-start | bytes 25165828 | tf_op jit(solution)/shard_map/while
  507.8 12.4 %copy-start.1 = (f32[2048,1024]{1,0:T(8,128)S(1)}, f32[2048,1024]{1,0:T(8,128)}, u32[]{:S(2)}) copy-start(f32[2048,1024]{1,0:T(8,128)} %get-tuple-element.292) | copy-start | bytes 25165828 | tf_op jit(solution)/shard_map/while
  550.9 12.4 %copy-start.1 = (f32[2048,1024]{1,0:T(8,128)S(1)}, f32[2048,1024]{1,0:T(8,128)}, u32[]{:S(2)}) copy-start(f32[2048,1024]{1,0:T(8,128)} %get-tuple-element.292) | copy-start | bytes 25165828 | tf_op jit(solution)/shard_map/while
  594.1 12.4 %copy-start.1 = (f32[2048,1024]{1,0:T(8,128)S(1)}, f32[2048,1024]{1,0:T(8,128)}, u32[]{:S(2)}) copy-start(f32[2048,1024]{1,0:T(8,128)} %get-tuple-element.292) | copy-start | bytes 25165828 | tf_op jit(solution)/shard_map/while
  637.2 12.4 %copy-start.1 = (f32[2048,1024]{1,0:T(8,128)S(1)}, f32[2048,1024]{1,0:T(8,128)}, u32[]{:S(2)}) copy-start(f32[2048,1024]{1,0:T(8,128)} %get-tuple-element.292) | copy-start | bytes 25165828 | tf_op jit(solution)/shard_map/while
  680.3 12.4 %copy-start.1 = (f32[2048,1024]{1,0:T(8,128)S(1)}, f32[2048,1024]{1,0:T(8,128)}, u32[]{:S(2)}) copy-start(f32[2048,1024]{1,0:T(8,128)} %get-tuple-element.292) | copy-start | bytes 25165828 | tf_op jit(solution)/shard_map/while
  723.4 12.4 %copy-start.1 = (f32[2048,1024]{1,0:T(8,128)S(1)}, f32[2048,1024]{1,0:T(8,128)}, u32[]{:S(2)}) copy-start(f32[2048,1024]{1,0:T(8,128)} %get-tuple-element.292) | copy-start | bytes 25165828 | tf_op jit(solution)/shard_map/while
  766.5 12.4 %copy-start.1 = (f32[2048,1024]{1,0:T(8,128)S(1)}, f32[2048,1024]{1,0:T(8,128)}, u32[]{:S(2)}) copy-start(f32[2048,1024]{1,0:T(8,128)} %get-tuple-element.292) | copy-start | bytes 25165828 | tf_op jit(solution)/shard_map/while
  (26 other events, 142.9 us)
Sparse Core Ops, SparseCore 0:
  94.8 27.5 all-gather.1
where the time goes:
time: 856 us; the launch traced here: 855 us
  other arithmetic  436 us (51%)
  matrix products  131 us (15%)
  local copies, waits for them, and re-layouts  124 us (14%)
  blocking collectives  123 us (14%)
  waiting for transfers between devices  16.7 us (2%)
  between operations  14.1 us (2%)
  loops' own time  10.5 us (1%)
    another operation x32, other arithmetic, advance(): stacked = jnp.stack(term_list)  431 us
    dot_general x16, matrix products, advance(): jnp.einsum('grc,cm->grm', stacked, filtered_cols, preferred_element_type=...  127 us
    while x112, local copies, waits for them, and re-layouts  104 us
    psum x1, blocking collectives, per_device(): filtered = lax.psum(partial_value, 'pcol').astype(jnp.bfloat16)  82.8 us
    psum x1, blocking collectives, per_device(): spectra = lax.psum(partial_spectra.reshape(L, -1), ('prow', 'pcol'))  40.1 us
  transfers between devices with their start and end apart: 1, of which 1 were waited for; matrix products, arithmetic and copies ran while one was open for 1% of the time, Pallas kernels for 0%

commit v1 on v0

--- a/solution.py
+++ b/solution.py
@@ -9,6 +9,11 @@
 GROUP = 4
 
 
+def carry_pairs_all(mat):
+    z1 = jnp.sum(lax.all_gather(mat, axis_name="pcol"), axis=0)
+    return z1
+
+
 def next_legendre(previous, current, cosine, degree):
     return ((2.0 * degree - 1.0) * cosine * current - (degree - 1.0) * previous) / degree
 
@@ -16,7 +21,7 @@
 def per_device(inverse_cov, cosines, sky_maps):
     cols_here = inverse_cov.shape[1]
     partial_value = jnp.dot(inverse_cov, sky_maps, preferred_element_type=jnp.float32)
-    filtered = lax.psum(partial_value, "pcol").astype(jnp.bfloat16)
+    filtered = carry_pairs_all(partial_value).astype(jnp.bfloat16)
     column_index = lax.axis_index("pcol")
     full_maps = lax.all_gather(filtered, "prow", axis=0, tiled=True)
     filtered_cols = lax.dynamic_slice_in_dim(full_maps, column_index * cols_here, cols_here, 0)

time: 856 us -> 981 us (1.15)
  waiting for transfers between devices: 16.7 us -> 196 us
  blocking collectives: 123 us -> 40.1 us
  local copies, waits for them, and re-layouts: 124 us -> 145 us
    all_gather x0 -> x1, waiting for transfers between devices: none -> 179 us  [carry_pairs_all(): z1 = jnp.sum(lax.all_gather(mat, axis_name='pcol'), axis=0)]
    psum x1 -> x0, blocking collectives: 82.8 us -> none  [per_device(): filtered = lax.psum(partial_value, 'pcol').astype(jnp.bfloat16)]
    unnamed x3 -> x8, local copies, waits for them, and re-layouts: 9.44 us -> 30.5 us
  transfers between devices with their start and end apart: 1 -> 2, of which waited for: 1 -> 2; matrix products, arithmetic and copies ran while one was open for 1% -> 1% of each run, Pallas kernels for 0% -> 0%
where the time goes in v1:
time: 981 us; the launch traced here: 980 us
  other arithmetic  444 us (45%)
  waiting for transfers between devices  196 us (20%)
  local copies, waits for them, and re-layouts  145 us (15%)
  matrix products  132 us (13%)
  blocking collectives  40.1 us (4%)
  between operations  14.1 us (1%)
    another operation x32, other arithmetic, advance(): stacked = jnp.stack(term_list)  431 us
    all_gather x1, waiting for transfers between devices, carry_pairs_all(): z1 = jnp.sum(lax.all_gather(mat, axis_name='pcol'), axis=0)  179 us
    dot_general x16, matrix products, advance(): jnp.einsum('grc,cm->grm', stacked, filtered_cols, preferred_element_type=...  127 us
    while x112, local copies, waits for them, and re-layouts  104 us
    psum x1, blocking collectives, per_device(): spectra = lax.psum(partial_spectra.reshape(L, -1), ('prow', 'pcol'))  40.1 us
    unnamed x8, local copies, waits for them, and re-layouts  30.5 us
  transfers between devices with their start and end apart: 2, of which 2 were waited for; matrix products, arithmetic and copies ran while one was open for 1% of the time, Pallas kernels for 0%

profile of v1, /device:TPU:0, one launch (start us, length us, event | category | flops | bytes accessed | tf_op | source)
XLA Modules:
  0.0 980.5 jit_solution(6749792837446851162)
XLA Ops:
  13.1 178.9 %all-gather.6.cloned.1.call-done = f32[16384,192]{0,1:T(8,128)} async-done(((f32[2048,192]{0,1:T(8,128)}), f32[16384,192]{0,1:T(8,128)}) %all-gather.6.cloned.1.call-update) | async-done | bytes 12582928 | tf_op jit(solution)/shard_map/all_gather | solution.py:13
  192.1 21.0 %copy.5 = f32[24,8,8,2048]{3,2,1,0:T(8,128)} copy(f32[24,8,8,2048]{3,1,2,0:T(8,128)} %bitcast.54) | data formatting | bytes 25165824
  231.7 16.9 %all-gather.4.cloned.1.call-done = bf16[8192,192]{0,1:T(8,128)(2,1)} async-done(((bf16[2048,192]{0,1:T(8,128)(2,1)}), bf16[8192,192]{0,1:T(8,128)(2,1)}) %all-gather.4.cloned.1.call-update) | async-done | bytes 3145744 | tf_op jit(solution)/shard_map/all_gather | solution.py:26
  249.7 683.9 %while.18 = (s32[]{:T(128)}, f32[2048,1024]{1,0:T(8,128)}, f32[2048,1024]{1,0:T(8,128)}, f32[16,4,192]{2,1,0:T(4,128)S(1)}, s32[16]{0:T(128)S(1)}, /*index=5*/f3...) while((s32[]{:T(128)}, f32[2048,1024]{1,0:T(8,128)}, ...), condition=%wide.region_3.4_spmd.clone, body=%wide.region_1.3_spmd.clone.sunk | while | flops 3325034496 | bytes 194916608 | solution.py:49
  288.9 12.4 %convert_bitcast_fusion.6 = (bf16[1,2048,1024]{2,1,0:T(8,128)(2,1)S(1)}, f32[2048,1024]{1,0:T(8,128)S(1)}, bf16[1,2048,1024]{2,1,0:T(8,128)(2,1)}) fusion(f32[]{:T(128)} %bitcast.46, f32[]{:T(128)S(6)} %sub.98, f32[]{:T(128)} %bitcast.47, f32[2048,1024]{1,0:T(8,128)} %get-tuple-element.271, f32[]{:T(128)S(6)} %sub.99, f32[]{:T(128)} %bitcast.48, ...), kind=kLoop, calls=%fused_computation.16.clone.1 | loop fusion | flops 37748736 | bytes 41943076 | tf_op jit(solution)/shard_map/while/body/eval_jaxpr/stack | solution.py:42
  301.4 14.8 %convert_bitcast_fusion.7 = (bf16[1,2048,1024]{2,1,0:T(8,128)(2,1)}, f32[2048,1024]{1,0:T(8,128)}, bf16[1,2048,1024]{2,1,0:T(8,128)(2,1)}) fusion(f32[]{:T(128)} %bitcast.49, f32[]{:T(128)} %bitcast.47, f32[2048,1024]{1,0:T(8,128)} %get-tuple-element.271, f32[]{:T(128)S(6)} %sub.99, f32[]{:T(128)} %bitcast.48, f32[2048,1024]{1,0:T(8,128)} %get-tuple-element.270, ...), kind=kLoop, calls=%fused_computation.15.clone.1 | loop fusion | flops 37748736 | bytes 50331684 | tf_op jit(solution)/shard_map/while/body/eval_jaxpr/stack | solution.py:42
  332.0 12.4 %convert_bitcast_fusion.6 = (bf16[1,2048,1024]{2,1,0:T(8,128)(2,1)S(1)}, f32[2048,1024]{1,0:T(8,128)S(1)}, bf16[1,2048,1024]{2,1,0:T(8,128)(2,1)}) fusion(f32[]{:T(128)} %bitcast.46, f32[]{:T(128)S(6)} %sub.98, f32[]{:T(128)} %bitcast.47, f32[2048,1024]{1,0:T(8,128)} %get-tuple-element.271, f32[]{:T(128)S(6)} %sub.99, f32[]{:T(128)} %bitcast.48, ...), kind=kLoop, calls=%fused_computation.16.clone.1 | loop fusion | flops 37748736 | bytes 41943076 | tf_op jit(solution)/shard_map/while/body/eval_jaxpr/stack | solution.py:42
  344.4 14.8 %convert_bitcast_fusion.7 = (bf16[1,2048,1024]{2,1,0:T(8,128)(2,1)}, f32[2048,1024]{1,0:T(8,128)}, bf16[1,2048,1024]{2,1,0:T(8,128)(2,1)}) fusion(f32[]{:T(128)} %bitcast.49, f32[]{:T(128)} %bitcast.47, f32[2048,1024]{1,0:T(8,128)} %get-tuple-element.271, f32[]{:T(128)S(6)} %sub.99, f32[]{:T(128)} %bitcast.48, f32[2048,1024]{1,0:T(8,128)} %get-tuple-element.270, ...), kind=kLoop, calls=%fused_computation.15.clone.1 | loop fusion | flops 37748736 | bytes 50331684 | tf_op jit(solution)/shard_map/while/body/eval_jaxpr/stack | solution.py:42
  375.0 12.4 %convert_bitcast_fusion.6 = (bf16[1,2048,1024]{2,1,0:T(8,128)(2,1)S(1)}, f32[2048,1024]{1,0:T(8,128)S(1)}, bf16[1,2048,1024]{2,1,0:T(8,128)(2,1)}) fusion(f32[]{:T(128)} %bitcast.46, f32[]{:T(128)S(6)} %sub.98, f32[]{:T(128)} %bitcast.47, f32[2048,1024]{1,0:T(8,128)} %get-tuple-element.271, f32[]{:T(128)S(6)} %sub.99, f32[]{:T(128)} %bitcast.48, ...), kind=kLoop, calls=%fused_computation.16.clone.1 | loop fusion | flops 37748736 | bytes 41943076 | tf_op jit(solution)/shard_map/while/body/eval_jaxpr/stack | solution.py:42
  387.5 14.8 %convert_bitcast_fusion.7 = (bf16[1,2048,1024]{2,1,0:T(8,128)(2,1)}, f32[2048,1024]{1,0:T(8,128)}, bf16[1,2048,1024]{2,1,0:T(8,128)(2,1)}) fusion(f32[]{:T(128)} %bitcast.49, f32[]{:T(128)} %bitcast.47, f32[2048,1024]{1,0:T(8,128)} %get-tuple-element.271, f32[]{:T(128)S(6)} %sub.99, f32[]{:T(128)} %bitcast.48, f32[2048,1024]{1,0:T(8,128)} %get-tuple-element.270, ...), kind=kLoop, calls=%fused_computation.15.clone.1 | loop fusion | flops 37748736 | bytes 50331684 | tf_op jit(solution)/shard_map/while/body/eval_jaxpr/stack | solution.py:42
  418.1 12.4 %convert_bitcast_fusion.6 = (bf16[1,2048,1024]{2,1,0:T(8,128)(2,1)S(1)}, f32[2048,1024]{1,0:T(8,128)S(1)}, bf16[1,2048,1024]{2,1,0:T(8,128)(2,1)}) fusion(f32[]{:T(128)} %bitcast.46, f32[]{:T(128)S(6)} %sub.98, f32[]{:T(128)} %bitcast.47, f32[2048,1024]{1,0:T(8,128)} %get-tuple-element.271, f32[]{:T(128)S(6)} %sub.99, f32[]{:T(128)} %bitcast.48, ...), kind=kLoop, calls=%fused_computation.16.clone.1 | loop fusion | flops 37748736 | bytes 41943076 | tf_op jit(solution)/shard_map/while/body/eval_jaxpr/stack | solution.py:42
  430.5 14.8 %convert_bitcast_fusion.7 = (bf16[1,2048,1024]{2,1,0:T(8,128)(2,1)}, f32[2048,1024]{1,0:T(8,128)}, bf16[1,2048,1024]{2,1,0:T(8,128)(2,1)}) fusion(f32[]{:T(128)} %bitcast.49, f32[]{:T(128)} %bitcast.47, f32[2048,1024]{1,0:T(8,128)} %get-tuple-element.271, f32[]{:T(128)S(6)} %sub.99, f32[]{:T(128)} %bitcast.48, f32[2048,1024]{1,0:T(8,128)} %get-tuple-element.270, ...), kind=kLoop, calls=%fused_computation.15.clone.1 | loop fusion | flops 37748736 | bytes 50331684 | tf_op jit(solution)/shard_map/while/body/eval_jaxpr/stack | solution.py:42
  473.6 14.8 %convert_bitcast_fusion.7 = (bf16[1,2048,1024]{2,1,0:T(8,128)(2,1)}, f32[2048,1024]{1,0:T(8,128)}, bf16[1,2048,1024]{2,1,0:T(8,128)(2,1)}) fusion(f32[]{:T(128)} %bitcast.49, f32[]{:T(128)} %bitcast.47, f32[2048,1024]{1,0:T(8,128)} %get-tuple-element.271, f32[]{:T(128)S(6)} %sub.99, f32[]{:T(128)} %bitcast.48, f32[2048,1024]{1,0:T(8,128)} %get-tuple-element.270, ...), kind=kLoop, calls=%fused_computation.15.clone.1 | loop fusion | flops 37748736 | bytes 50331684 | tf_op jit(solution)/shard_map/while/body/eval_jaxpr/stack | solution.py:42
  516.6 14.8 %convert_bitcast_fusion.7 = (bf16[1,2048,1024]{2,1,0:T(8,128)(2,1)}, f32[2048,1024]{1,0:T(8,128)}, bf16[1,2048,1024]{2,1,0:T(8,128)(2,1)}) fusion(f32[]{:T(128)} %bitcast.49, f32[]{:T(128)} %bitcast.47, f32[2048,1024]{1,0:T(8,128)} %get-tuple-element.271, f32[]{:T(128)S(6)} %sub.99, f32[]{:T(128)} %bitcast.48, f32[2048,1024]{1,0:T(8,128)} %get-tuple-element.270, ...), kind=kLoop, calls=%fused_computation.15.clone.1 | loop fusion | flops 37748736 | bytes 50331684 | tf_op jit(solution)/shard_map/while/body/eval_jaxpr/stack | solution.py:42
  559.7 14.8 %convert_bitcast_fusion.7 = (bf16[1,2048,1024]{2,1,0:T(8,128)(2,1)}, f32[2048,1024]{1,0:T(8,128)}, bf16[1,2048,1024]{2,1,0:T(8,128)(2,1)}) fusion(f32[]{:T(128)} %bitcast.49, f32[]{:T(128)} %bitcast.47, f32[2048,1024]{1,0:T(8,128)} %get-tuple-element.271, f32[]{:T(128)S(6)} %sub.99, f32[]{:T(128)} %bitcast.48, f32[2048,1024]{1,0:T(8,128)} %get-tuple-element.270, ...), kind=kLoop, calls=%fused_computation.15.clone.1 | loop fusion | flops 37748736 | bytes 50331684 | tf_op jit(solution)/shard_map/while/body/eval_jaxpr/stack | solution.py:42
  602.8 14.8 %convert_bitcast_fusion.7 = (bf16[1,2048,1024]{2,1,0:T(8,128)(2,1)}, f32[2048,1024]{1,0:T(8,128)}, bf16[1,2048,1024]{2,1,0:T(8,128)(2,1)}) fusion(f32[]{:T(128)} %bitcast.49, f32[]{:T(128)} %bitcast.47, f32[2048,1024]{1,0:T(8,128)} %get-tuple-element.271, f32[]{:T(128)S(6)} %sub.99, f32[]{:T(128)} %bitcast.48, f32[2048,1024]{1,0:T(8,128)} %get-tuple-element.270, ...), kind=kLoop, calls=%fused_computation.15.clone.1 | loop fusion | flops 37748736 | bytes 50331684 | tf_op jit(solution)/shard_map/while/body/eval_jaxpr/stack | solution.py:42
  645.8 14.8 %convert_bitcast_fusion.7 = (bf16[1,2048,1024]{2,1,0:T(8,128)(2,1)}, f32[2048,1024]{1,0:T(8,128)}, bf16[1,2048,1024]{2,1,0:T(8,128)(2,1)}) fusion(f32[]{:T(128)} %bitcast.49, f32[]{:T(128)} %bitcast.47, f32[2048,1024]{1,0:T(8,128)} %get-tuple-element.271, f32[]{:T(128)S(6)} %sub.99, f32[]{:T(128)} %bitcast.48, f32[2048,1024]{1,0:T(8,128)} %get-tuple-element.270, ...), kind=kLoop, calls=%fused_computation.15.clone.1 | loop fusion | flops 37748736 | bytes 50331684 | tf_op jit(solution)/shard_map/while/body/eval_jaxpr/stack | solution.py:42
  688.9 14.8 %convert_bitcast_fusion.7 = (bf16[1,2048,1024]{2,1,0:T(8,128)(2,1)}, f32[2048,1024]{1,0:T(8,128)}, bf16[1,2048,1024]{2,1,0:T(8,128)(2,1)}) fusion(f32[]{:T(128)} %bitcast.49, f32[]{:T(128)} %bitcast.47, f32[2048,1024]{1,0:T(8,128)} %get-tuple-element.271, f32[]{:T(128)S(6)} %sub.99, f32[]{:T(128)} %bitcast.48, f32[2048,1024]{1,0:T(8,128)} %get-tuple-element.270, ...), kind=kLoop, calls=%fused_computation.15.clone.1 | loop fusion | flops 37748736 | bytes 50331684 | tf_op jit(solution)/shard_map/while/body/eval_jaxpr/stack | solution.py:42
  731.9 14.8 %convert_bitcast_fusion.7 = (bf16[1,2048,1024]{2,1,0:T(8,128)(2,1)}, f32[2048,1024]{1,0:T(8,128)}, bf16[1,2048,1024]{2,1,0:T(8,128)(2,1)}) fusion(f32[]{:T(128)} %bitcast.49, f32[]{:T(128)} %bitcast.47, f32[2048,1024]{1,0:T(8,128)} %get-tuple-element.271, f32[]{:T(128)S(6)} %sub.99, f32[]{:T(128)} %bitcast.48, f32[2048,1024]{1,0:T(8,128)} %get-tuple-element.270, ...), kind=kLoop, calls=%fused_computation.15.clone.1 | loop fusion | flops 37748736 | bytes 50331684 | tf_op jit(solution)/shard_map/while/body/eval_jaxpr/stack | solution.py:42
  775.0 14.8 %convert_bitcast_fusion.7 = (bf16[1,2048,1024]{2,1,0:T(8,128)(2,1)}, f32[2048,1024]{1,0:T(8,128)}, bf16[1,2048,1024]{2,1,0:T(8,128)(2,1)}) fusion(f32[]{:T(128)} %bitcast.49, f32[]{:T(128)} %bitcast.47, f32[2048,1024]{1,0:T(8,128)} %get-tuple-element.271, f32[]{:T(128)S(6)} %sub.99, f32[]{:T(128)} %bitcast.48, f32[2048,1024]{1,0:T(8,128)} %get-tuple-element.270, ...), kind=kLoop, calls=%fused_computation.15.clone.1 | loop fusion | flops 37748736 | bytes 50331684 | tf_op jit(solution)/shard_map/while/body/eval_jaxpr/stack | solution.py:42
  818.0 14.8 %convert_bitcast_fusion.7 = (bf16[1,2048,1024]{2,1,0:T(8,128)(2,1)}, f32[2048,1024]{1,0:T(8,128)}, bf16[1,2048,1024]{2,1,0:T(8,128)(2,1)}) fusion(f32[]{:T(128)} %bitcast.49, f32[]{:T(128)} %bitcast.47, f32[2048,1024]{1,0:T(8,128)} %get-tuple-element.271, f32[]{:T(128)S(6)} %sub.99, f32[]{:T(128)} %bitcast.48, f32[2048,1024]{1,0:T(8,128)} %get-tuple-element.270, ...), kind=kLoop, calls=%fused_computation.15.clone.1 | loop fusion | flops 37748736 | bytes 50331684 | tf_op jit(solution)/shard_map/while/body/eval_jaxpr/stack | solution.py:42
  861.1 14.8 %convert_bitcast_fusion.7 = (bf16[1,2048,1024]{2,1,0:T(8,128)(2,1)}, f32[2048,1024]{1,0:T(8,128)}, bf16[1,2048,1024]{2,1,0:T(8,128)(2,1)}) fusion(f32[]{:T(128)} %bitcast.49, f32[]{:T(128)} %bitcast.47, f32[2048,1024]{1,0:T(8,128)} %get-tuple-element.271, f32[]{:T(128)S(6)} %sub.99, f32[]{:T(128)} %bitcast.48, f32[2048,1024]{1,0:T(8,128)} %get-tuple-element.270, ...), kind=kLoop, calls=%fused_computation.15.clone.1 | loop fusion | flops 37748736 | bytes 50331684 | tf_op jit(solution)/shard_map/while/body/eval_jaxpr/stack | solution.py:42
  904.1 14.8 %convert_bitcast_fusion.7 = (bf16[1,2048,1024]{2,1,0:T(8,128)(2,1)}, f32[2048,1024]{1,0:T(8,128)}, bf16[1,2048,1024]{2,1,0:T(8,128)(2,1)}) fusion(f32[]{:T(128)} %bitcast.49, f32[]{:T(128)} %bitcast.47, f32[2048,1024]{1,0:T(8,128)} %get-tuple-element.271, f32[]{:T(128)S(6)} %sub.99, f32[]{:T(128)} %bitcast.48, f32[2048,1024]{1,0:T(8,128)} %get-tuple-element.270, ...), kind=kLoop, calls=%fused_computation.15.clone.1 | loop fusion | flops 37748736 | bytes 50331684 | tf_op jit(solution)/shard_map/while/body/eval_jaxpr/stack | solution.py:42
  933.6 40.1 %psum.7 = f32[64,192]{1,0:T(8,128)} all-reduce(f32[64,192]{1,0:T(8,128)S(1)} %reshape.51), channel_id=1, replica_groups=mesh['prow'=4,'pcol'=8] {'prow','pcol'}, use_global_device_ids=true, to_apply=%region_4.5 | all-reduce | flops 12288 | bytes 98304 | tf_op jit(solution)/shard_map/psum | solution.py:52
  (208 shorter events, 427.4 us)
Async XLA Ops:
  7.2 184.9 %all-gather.6.cloned.1.call-start = ((), (), s32[]{:S(2)}) async-start(), calls=%async_computation.1 | async-start | bytes 14155776 | tf_op jit(solution)/shard_map/all_gather | solution.py:13
  13.1 235.5 %all-gather.4.cloned.1.call-start = ((), (), s32[]{:S(2)}) async-start(), calls=%async_computation | async-start | bytes 3932160 | tf_op jit(solution)/shard_map/all_gather | solution.py:26
  221.8 8.5 copy-start.5
  250.9 10.9 %copy-start.2 = (f32[2048,1024]{1,0:T(8,128)S(1)}, f32[2048,1024]{1,0:T(8,128)}, u32[]{:S(2)}) copy-start(f32[2048,1024]{1,0:T(8,128)} %get-tuple-element.292) | copy-start | bytes 25165828 | tf_op jit(solution)/shard_map/while
  288.9 12.4 %copy-start.2 = (f32[2048,1024]{1,0:T(8,128)S(1)}, f32[2048,1024]{1,0:T(8,128)}, u32[]{:S(2)}) copy-start(f32[2048,1024]{1,0:T(8,128)} %get-tuple-element.292) | copy-start | bytes 25165828 | tf_op jit(solution)/shard_map/while
  332.0 12.4 %copy-start.2 = (f32[2048,1024]{1,0:T(8,128)S(1)}, f32[2048,1024]{1,0:T(8,128)}, u32[]{:S(2)}) copy-start(f32[2048,1024]{1,0:T(8,128)} %get-tuple-element.292) | copy-start | bytes 25165828 | tf_op jit(solution)/shard_map/while
  375.0 12.4 %copy-start.2 = (f32[2048,1024]{1,0:T(8,128)S(1)}, f32[2048,1024]{1,0:T(8,128)}, u32[]{:S(2)}) copy-start(f32[2048,1024]{1,0:T(8,128)} %get-tuple-element.292) | copy-start | bytes 25165828 | tf_op jit(solution)/shard_map/while
  418.1 12.4 %copy-start.2 = (f32[2048,1024]{1,0:T(8,128)S(1)}, f32[2048,1024]{1,0:T(8,128)}, u32[]{:S(2)}) copy-start(f32[2048,1024]{1,0:T(8,128)} %get-tuple-element.292) | copy-start | bytes 25165828 | tf_op jit(solution)/shard_map/while
  461.1 12.4 %copy-start.2 = (f32[2048,1024]{1,0:T(8,128)S(1)}, f32[2048,1024]{1,0:T(8,128)}, u32[]{:S(2)}) copy-start(f32[2048,1024]{1,0:T(8,128)} %get-tuple-element.292) | copy-start | bytes 25165828 | tf_op jit(solution)/shard_map/while
  488.4 6.5 copy-start.4
  504.2 12.4 %copy-start.2 = (f32[2048,1024]{1,0:T(8,128)S(1)}, f32[2048,1024]{1,0:T(8,128)}, u32[]{:S(2)}) copy-start(f32[2048,1024]{1,0:T(8,128)} %get-tuple-element.292) | copy-start | bytes 25165828 | tf_op jit(solution)/shard_map/while
  531.5 6.5 copy-start.4
  547.3 12.4 %copy-start.2 = (f32[2048,1024]{1,0:T(8,128)S(1)}, f32[2048,1024]{1,0:T(8,128)}, u32[]{:S(2)}) copy-start(f32[2048,1024]{1,0:T(8,128)} %get-tuple-element.292) | copy-start | bytes 25165828 | tf_op jit(solution)/shard_map/while
  574.5 6.5 copy-start.4
  590.3 12.4 %copy-start.2 = (f32[2048,1024]{1,0:T(8,128)S(1)}, f32[2048,1024]{1,0:T(8,128)}, u32[]{:S(2)}) copy-start(f32[2048,1024]{1,0:T(8,128)} %get-tuple-element.292) | copy-start | bytes 25165828 | tf_op jit(solution)/shard_map/while
  617.6 6.5 copy-start.4
  633.4 12.4 %copy-start.2 = (f32[2048,1024]{1,0:T(8,128)S(1)}, f32[2048,1024]{1,0:T(8,128)}, u32[]{:S(2)}) copy-start(f32[2048,1024]{1,0:T(8,128)} %get-tuple-element.292) | copy-start | bytes 25165828 | tf_op jit(solution)/shard_map/while
  676.4 12.4 %copy-start.2 = (f32[2048,1024]{1,0:T(8,128)S(1)}, f32[2048,1024]{1,0:T(8,128)}, u32[]{:S(2)}) copy-start(f32[2048,1024]{1,0:T(8,128)} %get-tuple-element.292) | copy-start | bytes 25165828 | tf_op jit(solution)/shard_map/while
  719.5 12.4 %copy-start.2 = (f32[2048,1024]{1,0:T(8,128)S(1)}, f32[2048,1024]{1,0:T(8,128)}, u32[]{:S(2)}) copy-start(f32[2048,1024]{1,0:T(8,128)} %get-tuple-element.292) | copy-start | bytes 25165828 | tf_op jit(solution)/shard_map/while
  762.5 12.4 %copy-start.2 = (f32[2048,1024]{1,0:T(8,128)S(1)}, f32[2048,1024]{1,0:T(8,128)}, u32[]{:S(2)}) copy-start(f32[2048,1024]{1,0:T(8,128)} %get-tuple-element.292) | copy-start | bytes 25165828 | tf_op jit(solution)/shard_map/while
  805.6 12.4 %copy-start.2 = (f32[2048,1024]{1,0:T(8,128)S(1)}, f32[2048,1024]{1,0:T(8,128)}, u32[]{:S(2)}) copy-start(f32[2048,1024]{1,0:T(8,128)} %get-tuple-element.292) | copy-start | bytes 25165828 | tf_op jit(solution)/shard_map/while
  848.7 12.4 %copy-start.2 = (f32[2048,1024]{1,0:T(8,128)S(1)}, f32[2048,1024]{1,0:T(8,128)}, u32[]{:S(2)}) copy-start(f32[2048,1024]{1,0:T(8,128)} %get-tuple-element.292) | copy-start | bytes 25165828 | tf_op jit(solution)/shard_map/while
  891.7 12.4 %copy-start.2 = (f32[2048,1024]{1,0:T(8,128)S(1)}, f32[2048,1024]{1,0:T(8,128)}, u32[]{:S(2)}) copy-start(f32[2048,1024]{1,0:T(8,128)} %get-tuple-element.292) | copy-start | bytes 25165828 | tf_op jit(solution)/shard_map/while
  933.5 40.1 %copy-start.1 = (bf16[1024,192]{0,1:T(8,128)(2,1)S(1)}, bf16[1024,192]{0,1:T(8,128)(2,1)}, u32[]{:S(2)}) copy-start(bf16[1024,192]{0,1:T(8,128)(2,1)} %param.7) | copy-start | bytes 1179652
  (29 other events, 162.4 us)
Sparse Core Ops, SparseCore 0:
  13.2 178.8 all-gather.5
  221.9 26.6 all-gather.3
